TPU v7x, 512 devices: a 8x2x16 block of a 8x8x16 slice. The times are simulated.
512 devices in a mesh: ga: 2 (over y), gx: 16 (over z), gy: 8 (over x), col: 2 (over core).
Axes of the slice: x: 8, y: 2, z: 16, core: 2. Of those that a mesh axis runs over, the one named last changes fastest.
The devices are a block of a 8x8x16 slice.
Arguments:
- pair_rep: bfloat16 [2, 640, 640, 128], P('ga', 'gx', 'gy'), parts along dimension 0, may hold values from -6 to 6
- pair_mask: int32 [2, 640, 640], P('ga', 'gx', 'gy'), parts along dimension 0, may hold values 0 or 1
- amax_history: float32 [2, 128], P(None, 'col'), may hold values from 0.3 to 3
- in_gain: float32 [128], replicated, may hold values from 0.5 to 1.5
- in_bias: float32 [128], replicated, may hold values from -3 to 3
- proj_weight: bfloat16 [128, 4, 128], P(None, None, 'col'), may hold values from -0.5 to 0.5
- gate_weight: bfloat16 [128, 128], P(None, 'col'), may hold values from -0.5 to 0.5
- out_gain: float32 [128], replicated, may hold values from 0.5 to 1.5
- out_bias: float32 [128], replicated, may hold values from -3 to 3
- out_weight: bfloat16 [128, 128], P(None, 'col'), may hold values from -0.5 to 0.5
Outputs:
- update: bfloat16 [2, 640, 640, 128], P('ga', 'gx', 'gy', 'col'), parts along dimension 0
- new_amax: float32 [4, 128], P('ga', 'col'), parts along dimension 0
There are 2 independent parts, one for each index of `ga`. A program takes and returns all parts, laid end to end along the dimension named above; an argument that names none is the same for every part. Nothing has to cross between parts.
All inputs are finite; a program needn't handle non-finite values. No bound on the sum of `pair_mask` on one device may be relied on, other than what follows from the above.
Results may differ from a plain program's by a relative error of at most 0.0065.
Values may be sent and summed in bfloat16 or wider, within the bound.
A program may use at most 128 MiB of HBM per device.

v0:
```python
import jax
import jax.numpy as jnp
from jax import lax
from jax.sharding import PartitionSpec as P

epsilon = 1e-05
format_limit = 448.0


def broadcast(block, axis, holder):
    block = jnp.where(lax.axis_index(axis) == holder, block, jnp.zeros_like(block))
    return lax.psum(block, axis)


def copy_for_each(array, axis):
    copies = jnp.broadcast_to(array, (lax.axis_size(axis), *array.shape))
    return lax.all_to_all(copies, axis, split_axis=0, concat_axis=0, tiled=True)


def joined_along(parts, dim):
    dims = list(parts.shape[1:])
    dims[dim] *= parts.shape[0]
    return jnp.moveaxis(parts, 0, dim).reshape(dims)


def gather_directly(array, axis, dim):
    parts = copy_for_each(array, axis)
    return joined_along(parts, dim)


def total_of_pieces(array, axis):
    parts = lax.all_gather(array, axis)
    return parts.max(axis=0)


def layer_norm(values, gain, bias):
    average = jnp.mean(values, axis=-1, keepdims=True)
    spread = jnp.mean(jnp.square(values - average), axis=-1, keepdims=True)
    return (values - average) * lax.rsqrt(spread + epsilon) * gain + bias


def crop_triangle(left_q, right_q):
    wide_rows = lax.all_gather(right_q, "gy", axis=2, tiled=True)
    row_ratio = lax.axis_size("gx") // lax.axis_size("gy")
    first_root = lax.axis_index("gy") * row_ratio
    received = [
        broadcast(wide_rows, "gx", first_root + offset_step) for offset_step in range(row_ratio)
    ]
    panel = jnp.concatenate(received, axis=1)
    return jnp.einsum(
        "cik,cjk->cij", gather_directly(left_q, "gy", 2), panel, preferred_element_type=jnp.float32
    )


def on_device(
    pair_rep,
    pair_mask,
    amax_history,
    in_gain,
    in_bias,
    proj_weight,
    gate_weight,
    out_gain,
    out_bias,
    out_weight,
):
    normed = layer_norm(pair_rep.astype(jnp.float32), in_gain, in_bias).astype(jnp.bfloat16)
    projected = jnp.einsum(
        "bikd,dsc->scbik", normed, proj_weight, preferred_element_type=jnp.float32
    )
    masking = pair_mask.astype(jnp.float32)[None]
    left_proj = masking * jax.nn.sigmoid(projected[1]) * projected[0]
    right_proj = masking * jax.nn.sigmoid(projected[3]) * projected[2]
    local_max = jnp.stack(
        [jnp.max(jnp.abs(left_proj), axis=(1, 2, 3)), jnp.max(jnp.abs(right_proj), axis=(1, 2, 3))]
    )
    new_amax = total_of_pieces(local_max, ("gx", "gy"))
    scales = amax_history / format_limit
    left_q = jnp.clip(
        left_proj / scales[0][:, None, None, None], -format_limit, format_limit
    ).astype(jnp.bfloat16)
    right_q = jnp.clip(
        right_proj / scales[1][:, None, None, None], -format_limit, format_limit
    ).astype(jnp.bfloat16)
    products = jnp.stack([crop_triangle(left_q[:, 0], right_q[:, 0])], axis=1)
    triangle = (products * (scales[0] * scales[1])[:, None, None, None]).astype(jnp.bfloat16)
    gathered = lax.all_gather(triangle, "col", axis=0, tiled=True).astype(jnp.float32)
    average = jnp.mean(gathered, axis=0, keepdims=True)
    spread = jnp.mean(jnp.square(gathered - average), axis=0, keepdims=True)
    tnorm = (
        (gathered - average) * lax.rsqrt(spread + epsilon) * out_gain[:, None, None, None]
        + out_bias[:, None, None, None]
    ).astype(jnp.bfloat16)
    mixing = jnp.einsum("cbij,cd->bijd", tnorm, out_weight, preferred_element_type=jnp.float32)
    gating = jax.nn.sigmoid(
        jnp.einsum("bijd,dc->bijc", normed, gate_weight, preferred_element_type=jnp.float32)
    )
    update = (gating * mixing).astype(jnp.bfloat16)
    return (update, new_amax)


def solution(mesh):
    placed = (
        P("ga", "gx", "gy", None),
        P("ga", "gx", "gy"),
        P(None, "col"),
        P(),
        P(),
        P(None, None, "col"),
        P(None, "col"),
        P(),
        P(),
        P(None, "col"),
    )
    return jax.shard_map(
        on_device,
        mesh=mesh,
        in_specs=placed,
        out_specs=(P("ga", "gx", "gy", "col"), P("ga", "col")),
        check_vma=False,
    )
```

profile of v0, /device:TPU:65, one launch (start us, length us, event | category | flops | bytes accessed | tf_op | source)
XLA Modules:
  0.0 403.0 jit_solution(6059494972928307105)
XLA Ops:
  7.2 0.0 copy-start
  7.2 0.0 copy-start.2
  7.2 0.0 copy-start.7
  7.2 0.0 copy-start.8
  7.2 0.1 all-gather.5.cloned.1.call-start
  7.3 0.7 broadcast_multiply_fusion.2
  8.0 0.7 convert_bitcast_fusion.1
  8.8 1.6 convert_reduce_fusion.1
  10.4 2.3 fusion.13
  12.7 0.0 copy-done
  12.7 0.0 copy-done.2
  12.7 0.0 copy-done.7
  12.7 0.0 copy-done.8
  12.8 2.1 convolution_bitcast_fusion
  14.9 0.0 copy-start.1
  14.9 2.3 fusion.45
  17.1 0.2 copy-done.1
  17.4 1.3 copy.23
  18.7 0.1 all-gather.5.cloned.1.call-update
  18.8 0.1 all-reduce.3.cloned.1.call-start
  18.8 117.4 %all-gather.5.cloned.1.call-done = bf16[64,40,640]{0,1,2:T(8,128)(2,1)} async-done(((bf16[64,40,80]{0,1,2:T(8,128)(2,1)}), bf16[64,40,640]{0,1,2:T(8,128)(2,1)}) %all-gather.5.cloned.1.call-update) | async-done | bytes 3276816 | tf_op jit(solution)/shard_map/all_gather | solution.py:43
  136.3 14.6 %copy.24 = bf16[64,40,640]{2,1,0:T(8,128)(2,1)S(1)} copy(bf16[64,40,640]{0,1,2:T(8,128)(2,1)} %all-gather.5.cloned.1.call-done) | data formatting | bytes 6553600 | tf_op jit(solution)/shard_map/all_gather | solution.py:43
  150.8 3.3 broadcast_select_fusion.1
  154.1 0.0 copy-start.4
  154.1 0.1 all-reduce.3.cloned.1.call-update
  154.2 1.0 copy-done.4
  155.2 0.4 copy.20
  155.6 3.0 broadcast_in_dim.2
  158.6 4.8 %all-to-all-start = ((bf16[8,64,40,80]{3,2,1,0:T(8,128)(2,1)}), bf16[8,64,40,80]{3,2,1,0:T(8,128)(2,1)}, u32[]{:S(2)}, u32[]{:S(2)}) async-start(bf16[8,64,40,80]{3,2,1,0:T(8,128)(2,1)} %broadcast_in_dim.2), calls=%async_computation | async-start | bytes 10485760 | tf_op jit(solution)/shard_map/all_to_all | solution.py:17
  163.5 0.0 copy-start.3
  163.5 0.0 copy-start.11
  163.5 3.5 fusion.37
  167.0 185.1 %all-gather.2 = f32[128,2,64]{2,1,0:T(2,128)S(1)} all-gather(f32[1,2,64]{2,1,0:T(2,128)S(1)} %maximum_bitcast_fusion), channel_id=3, replica_groups=mesh['ga'=2,'gx'=16,'gy'=8,'col'=2] {'gx','gy'}, dimensions={0}, use_global_device_ids=true | all-gather | bytes 66048 | tf_op jit(solution)/shard_map/all_gather | solution.py:32
  352.2 0.7 reduce_max.29
  352.9 0.0 copy-done.3
  352.9 0.0 copy-done.11
  352.9 2.3 fusion.19
  355.2 0.0 all-to-all-done
  355.2 10.9 %copy.21 = bf16[64,40,8,80]{3,2,1,0:T(8,128)(2,1)} copy(bf16[64,40,8,80]{3,1,0,2:T(8,128)(2,1)} %bitcast.10) | data formatting | bytes 6553600 | tf_op jit(solution)/shard_map/transpose | solution.py:23
  366.1 7.2 %reshape.236 = bf16[64,40,640]{2,1,0:T(8,128)(2,1)S(1)} reshape(bf16[64,40,8,80]{3,2,1,0:T(8,128)(2,1)} %copy.21) | data formatting | bytes 6553600 | tf_op jit(solution)/shard_map/reshape | solution.py:23
  373.3 0.0 all-reduce.3.cloned.1.call-done
  373.3 5.1 %fusion.23 = bf16[64,40,80]{2,1,0:T(8,128)(2,1)S(1)} fusion(bf16[64,40,640]{2,1,0:T(8,128)(2,1)S(1)} %reshape.236, bf16[64,40,640]{2,1,0:T(8,128)(2,1)} %get-tuple-element.4, bf16[64,40,640]{2,1,0:T(8,128)(2,1)} %get-tuple-element.5, f32[64]{0:T(128)S(1)} %fusion.58), kind=kOutput, calls=%fused_computation.30 | convolution fusion | flops 275660800 | bytes 10240256 | tf_op jit(solution)/shard_map/cik,cjk->cij/dot_general | solution.py:50
  378.4 14.5 %all-gather = bf16[128,40,80]{2,1,0:T(8,128)(2,1)S(1)} all-gather(bf16[64,40,80]{2,1,0:T(8,128)(2,1)S(1)} %fusion.23), channel_id=2, replica_groups=mesh['ga'=2,'gx'=16,'gy'=8,'col'=2] {'col'}, dimensions={0}, use_global_device_ids=true | all-gather | bytes 1228800 | tf_op jit(solution)/shard_map/all_gather | solution.py:87
  392.9 0.0 copy-start.9
  392.9 0.0 copy-start.10
  392.9 0.3 convert_reduce_fusion
  393.2 0.5 fusion.7
  393.7 0.0 copy-start.5
  393.7 0.0 copy-start.6
  393.7 0.0 copy-done.9
  393.7 0.0 copy-done.10
  393.7 0.5 fusion.27
  394.3 0.7 copy-done.5
  395.0 0.0 copy-done.6
  395.0 1.2 fusion.47
  (7 shorter events, 0.1 us)
Async XLA Ops:
  7.2 5.5 %copy-start = (bf16[128,4,64]{0,2,1:T(8,128)(2,1)S(1)}, bf16[128,4,64]{0,2,1:T(8,128)(2,1)}, u32[]{:S(2)}) copy-start(bf16[128,4,64]{0,2,1:T(8,128)(2,1)} %param.15) | copy-start | bytes 196612
  7.2 5.5 %copy-start.2 = (bf16[1,40,80,128]{3,2,1,0:T(8,128)(2,1)S(1)}, bf16[1,40,80,128]{3,2,1,0:T(8,128)(2,1)}, u32[]{:S(2)}) copy-start(bf16[1,40,80,128]{3,2,1,0:T(8,128)(2,1)} %param.10) | copy-start | bytes 2457604
  7.2 5.5 %copy-start.7 = (f32[128]{0:T(128)S(1)}, f32[128]{0:T(128)}, u32[]{:S(2)}) copy-start(f32[128]{0:T(128)} %param.14) | copy-start | bytes 1540
  7.2 5.5 %copy-start.8 = (f32[128]{0:T(128)S(1)}, f32[128]{0:T(128)}, u32[]{:S(2)}) copy-start(f32[128]{0:T(128)} %param.13) | copy-start | bytes 1540
  7.2 129.0 %all-gather.5.cloned.1.call-start = ((), (), s32[]{:S(2)}) async-start(), calls=%async_computation.1 | async-start | bytes 7372800 | tf_op jit(solution)/shard_map/all_gather | solution.py:43
  14.9 2.5 copy-start.1
  18.8 354.5 %all-reduce.3.cloned.1.call-start = ((), (), s32[]{:S(2)}) async-start(), calls=%async_computation.2 | async-start | bytes 13107200 | tf_op jit(solution)/shard_map/psum | solution.py:12
  154.1 1.1 copy-start.4
  158.6 196.6 %all-to-all-start = ((bf16[8,64,40,80]{3,2,1,0:T(8,128)(2,1)}), bf16[8,64,40,80]{3,2,1,0:T(8,128)(2,1)}, u32[]{:S(2)}, u32[]{:S(2)}) async-start(bf16[8,64,40,80]{3,2,1,0:T(8,128)(2,1)} %broadcast_in_dim.2), calls=%async_computation | async-start | bytes 10485760 | tf_op jit(solution)/shard_map/all_to_all | solution.py:17
  163.5 189.4 %copy-start.3 = (bf16[1,40,80,128]{3,2,1,0:T(8,128)(2,1)S(1)}, bf16[1,40,80,128]{3,2,1,0:T(8,128)(2,1)}, u32[]{:S(2)}) copy-start(bf16[1,40,80,128]{3,2,1,0:T(8,128)(2,1)} %param.10) | copy-start | bytes 2457604
  163.5 189.4 %copy-start.11 = (bf16[128,64]{0,1:T(8,128)(2,1)S(1)}, bf16[128,64]{0,1:T(8,128)(2,1)}, u32[]{:S(2)}) copy-start(bf16[128,64]{0,1:T(8,128)(2,1)} %param.16) | copy-start | bytes 49156
  392.9 0.8 copy-start.9
  392.9 0.8 copy-start.10
  393.7 1.3 copy-start.5
  393.7 1.3 copy-start.6
Sparse Core Ops, SparseCore 0:
  18.9 117.3 all-gather.4
  154.3 179.9 all-reduce.2
where the time goes:
time: 404 us; the launch traced here: 403 us
  blocking collectives  200 us (50%)
  waiting for transfers between devices  118 us (29%)
  local copies, waits for them, and re-layouts  39.4 us (10%)
  other arithmetic  16.5 us (4%)
  between operations  14.3 us (4%)
  matrix products  10.7 us (3%)
  starting transfers between devices  4.97 us (1%)
    all_gather x1, blocking collectives, total_of_pieces(): parts = lax.all_gather(array, axis)  185 us
    all_gather x1, waiting for transfers between devices, crop_triangle(): wide_rows = lax.all_gather(right_q, 'gy', axis=2, tiled=True)  117 us
    all_gather x1, local copies, waits for them, and re-layouts, crop_triangle(): wide_rows = lax.all_gather(right_q, 'gy', axis=2, tiled=True)  14.6 us
    all_gather x1, blocking collectives, on_device(): lax.all_gather(triangle, 'col', axis=0, tiled=True).astype(jnp.float32)  14.5 us
    transpose x1, local copies, waits for them, and re-layouts, joined_along(): return jnp.moveaxis(parts, 0, dim).reshape(dims)  10.9 us
  transfers between devices with their start and end apart: 3, of which 1 were waited for; matrix products, arithmetic and copies ran while one was open for 7% of the time, Pallas kernels for 0%

commit v1 on v0

v1 whole, which is shorter than its diff:
```python
import functools

import jax
import jax.numpy as jnp
from jax import lax
from jax.experimental import pallas as pl
from jax.experimental.pallas import tpu as pltpu
from jax.sharding import PartitionSpec as P

epsilon = 1e-05
format_limit = 448.0
MESH = pl.DeviceIdType.MESH
f32, bf16 = jnp.float32, jnp.bfloat16


def block_transpose(parts):
    parts = list(parts)
    shape = parts[0].shape
    block = lax.broadcasted_iota(jnp.int32, shape, len(shape) - 1) // 16
    for bit in (4, 2, 1):
        low = (block & bit) == 0
        for a in range(8):
            if a & bit:
                continue
            x, y = parts[a], parts[a | bit]
            parts[a] = jnp.where(low, x, pltpu.roll(y, 16 * bit, 1))
            parts[a | bit] = jnp.where(low, pltpu.roll(x, 128 - 16 * bit, 1), y)
    return parts


def kernel(
    sizes,
    pair_ref,
    mask_ref,
    w_ref,
    inv_ref,
    back_ref,
    gain_ref,
    bias_ref,
    gate_w_ref,
    out_gain_ref,
    out_bias_ref,
    out_w_ref,
    out_ref,
    amax_ref,
    normed,
    gates,
    peak,
    xsend,
    xrecv,
    staged,
    ready,
    rhome,
    rmat,
    lhome,
    tsend,
    trecv,
    staged2,
    txsend,
    tfull,
    peak_x,
    peak_z,
    x_ss,
    x_rs,
    r_ss,
    r_rs,
    l_ss,
    l_rs,
    t_ss,
    t_rs,
    tx_ss,
    tx_rs,
    d_ss,
    d_rs,
    px_ss,
    px_rs,
    pz_ss,
    pz_rs,
):
    nz, nx, chunks = sizes
    z, x, core = lax.axis_index("gx"), lax.axis_index("gy"), lax.axis_index("col")
    other = 1 - core
    half = nz // 2

    def zp(d):
        return lax.rem(z + d, nz)

    def xp(d):
        return lax.rem(x + d, nx)

    sends = []

    def send(src, dst, ss, rs, target):
        copy = pltpu.make_async_remote_copy(
            src_ref=src,
            dst_ref=dst,
            send_sem=ss,
            recv_sem=rs,
            device_id=target,
            device_id_type=MESH,
        )
        copy.start()
        sends.append(copy)

    def arrived(dst, rs):
        pltpu.make_async_copy(dst, dst, rs).wait()

    barrier = pltpu.get_barrier_semaphore()
    for d in range(1, nx):
        pl.semaphore_signal(barrier, inc=1, device_id={"gy": xp(d)}, device_id_type=MESH)
    for d in range(1, nz):
        pl.semaphore_signal(barrier, inc=1, device_id={"gx": zp(d)}, device_id_type=MESH)
    pl.semaphore_signal(barrier, inc=1, device_id={"col": other}, device_id_type=MESH)

    far = nz // 4
    z_order = []
    for d in range(nz // 2, 0, -1):
        z_order.append(d)
        if nz - d != d:
            z_order.append(nz - d)
    x_order = []
    for d in range(nx // 2, 0, -1):
        x_order.append(d)
        if nx - d != d:
            x_order.append(nx - d)
    arc = [e % nz for e in range(1 - far, far)] + [lax.rem(far + half * core, nz)]
    own = far - 1

    for c in range(chunks):
        rows = pair_ref[8 * c : 8 * c + 8].reshape(640, 128).astype(f32)
        average = jnp.mean(rows, axis=-1, keepdims=True)
        centred = rows - average
        spread = jnp.mean(centred * centred, axis=-1, keepdims=True)
        flat = (centred * lax.rsqrt(spread + epsilon) * gain_ref[...] + bias_ref[...]).astype(bf16)
        normed[640 * c : 640 * c + 640, :] = flat
        proj = lax.dot_general(
            w_ref[...], flat, (((1,), (1,)), ((), ())), preferred_element_type=f32
        )
        both = mask_ref[c] * jax.nn.sigmoid(proj[128:]) * proj[:128]
        top = jnp.abs(both)
        top = jnp.maximum(
            jnp.maximum(
                jnp.maximum(top[:, :128], top[:, 128:256]),
                jnp.maximum(top[:, 256:384], top[:, 384:512]),
            ),
            top[:, 512:],
        )
        peak[...] = top if c == 0 else jnp.maximum(peak[...], top)
        quant = jnp.clip(both * inv_ref[...], -format_limit, format_limit).astype(bf16)
        xsend[c] = quant.reshape(8, 16, 640)
        xrecv[c, x] = xsend[c, x]
        if c == 0:
            pl.semaphore_wait(barrier, nx + nz - 1)
        for d in x_order:
            t = xp(d)
            send(xsend.at[c, t], xrecv.at[c, x], x_ss.at[c, d], x_rs.at[c, d], {"gy": t})

    for c in range(chunks):
        for d in x_order:
            arrived(xrecv.at[c, xp(nx - d)], x_rs.at[c, d])
        for g in range(5):
            parts = [xrecv[c, a, :, 128 * g : 128 * g + 128].astype(f32) for a in range(8)]
            for p, part in enumerate(block_transpose(parts)):
                staged[16 * (8 * g + p) : 16 * (8 * g + p) + 16, :] = part
        for r in range(16):
            tiles = [staged[pl.ds(16 * k + r, 8, stride=80), :] for k in range(5)]
            ready[r, c] = jnp.concatenate(tiles, axis=1).astype(bf16)
        rhome[c, z] = ready[8 + lax.rem(z, half), c]
        for d in z_order:
            t = zp(d)
            send(
                ready.at[8 + lax.rem(t, half), c],
                rhome.at[c, z],
                r_ss.at[c, d],
                r_rs.at[c, d],
                {"gx": t},
            )

    for c in range(chunks):
        for a, e in enumerate(arc):
            if a == own:
                lhome[c, a] = ready[lax.rem(z, half), c]
                continue
            t = zp(e)
            send(
                ready.at[lax.rem(t, half), c],
                lhome.at[c, a],
                l_ss.at[c, a],
                l_rs.at[c, a],
                {"gx": t},
            )

    tops = peak[...].reshape(8, 2, 8, 128)
    tops = jnp.concatenate([tops[:, 0].reshape(64, 128), tops[:, 1].reshape(64, 128)], axis=0)
    peak_x[x] = jnp.max(tops.T, axis=0, keepdims=True)
    for d in x_order:
        send(peak_x.at[x], peak_x.at[x], px_ss.at[d], px_rs.at[d], {"gy": xp(d)})
    for c in range(chunks):
        gates[640 * c : 640 * c + 640, :] = jax.nn.sigmoid(
            jnp.dot(normed[640 * c : 640 * c + 640, :], gate_w_ref[...], preferred_element_type=f32)
        )
    for d in x_order:
        arrived(peak_x.at[xp(nx - d)], px_rs.at[d])
    peak_z[z] = jnp.max(peak_x[...], axis=0)
    for d in z_order:
        send(peak_z.at[z], peak_z.at[z], pz_ss.at[d], pz_rs.at[d], {"gx": zp(d)})

    for c in range(chunks):
        for d in z_order:
            arrived(rhome.at[c, zp(nz - d)], r_rs.at[c, d])
        rmat[128 * c : 128 * c + 128, :] = rhome[c].astype(f32).reshape(128, 640).astype(bf16)

    for c in range(chunks):
        for a in range(len(arc)):
            if a != own:
                arrived(lhome.at[c, a], l_rs.at[c, a])
        left = lhome[c].astype(f32).reshape(64, 640).astype(bf16)
        product = lax.dot_general(
            left, rmat[...], (((1,), (1,)), ((), ())), preferred_element_type=f32
        )
        scaled = product * back_ref[x, lax.rem(z, half)]
        tsend[c] = scaled.reshape(8, 8, 640).astype(bf16)
        for a, e in enumerate(arc):
            if a == own:
                trecv[c, lax.rem(z, half)] = tsend[c, a]
                continue
            t = zp(nz - e)
            send(
                tsend.at[c, a],
                trecv.at[c, lax.rem(z, half)],
                t_ss.at[c, a],
                t_rs.at[c, a],
                {"gx": t},
            )

    def over_x(c):
        for a, e in enumerate(arc):
            if a != own:
                arrived(trecv.at[c, lax.rem(zp(e), half)], t_rs.at[c, a])
        for s in range(8):
            for j in range(5):
                staged2[pl.ds(8 * j + s, 8, stride=40), :] = trecv[
                    c, s, :, 128 * j : 128 * j + 128
                ].astype(f32)
        for g in range(5):
            parts = [staged2[8 * (8 * g + p) : 8 * (8 * g + p) + 8, :] for p in range(8)]
            for b, part in enumerate(block_transpose(parts)):
                txsend[c, b, :, 128 * g : 128 * g + 128] = part.astype(bf16)
        tfull[c, core, x] = txsend[c, x]
        for d in x_order:
            t = xp(d)
            send(txsend.at[c, t], tfull.at[c, core, x], tx_ss.at[c, d], tx_rs.at[c, d], {"gy": t})

    def over_core(c):
        for d in x_order:
            arrived(tfull.at[c, core, xp(nx - d)], tx_rs.at[c, d])
        send(tfull.at[c, core], tfull.at[c, core], d_ss.at[c], d_rs.at[c], {"col": other})

    def finish(c):
        arrived(tfull.at[c, other], d_rs.at[c])
        values = tfull[c].astype(f32).reshape(128, 640)
        average = jnp.mean(values, axis=0, keepdims=True)
        centred = values - average
        spread = jnp.mean(centred * centred, axis=0, keepdims=True)
        tnorm = (
            centred * lax.rsqrt(spread + epsilon) * out_gain_ref[...] + out_bias_ref[...]
        ).astype(bf16)
        mixing = lax.dot_general(
            tnorm, out_w_ref[...], (((0,), (0,)), ((), ())), preferred_element_type=f32
        )
        groups = mixing.reshape(8, 5, 2, 8, 64)
        gate = gates[640 * c : 640 * c + 640, :].reshape(8, 2, 5, 8, 64)
        for b in range(2):
            for j in range(5):
                out_ref[8 * c : 8 * c + 8, 40 * b + 8 * j : 40 * b + 8 * j + 8, :] = (
                    gate[:, b, j] * groups[:, j, b]
                ).astype(bf16)

    for step in range(chunks + 2):
        if step < chunks:
            over_x(step)
        if 0 <= step - 1 < chunks:
            over_core(step - 1)
        if 0 <= step - 2 < chunks:
            finish(step - 2)

    for d in z_order:
        arrived(peak_z.at[zp(nz - d)], pz_rs.at[d])
    tops = jnp.max(peak_z[...], axis=0)
    amax_ref[0:1, :] = tops[:, :64]
    amax_ref[1:2, :] = tops[:, 64:]

    for copy in sends:
        copy.wait_send()


def solution(mesh):
    nz, nx = mesh.shape["gx"], mesh.shape["gy"]

    def on_device(
        pair_rep,
        pair_mask,
        amax_history,
        in_gain,
        in_bias,
        proj_weight,
        gate_weight,
        out_gain,
        out_bias,
        out_weight,
    ):
        _, ni, nj, width = pair_rep.shape
        held = proj_weight.shape[2]
        chunks = ni // 8
        assert nx == 8 and nz == 16 and nj == 80 and width == 128 and held == 64
        lanes = 8 * nj
        ordered = proj_weight.transpose(1, 2, 0).reshape(2, 2, nx, 8, width)
        weights = ordered.transpose(1, 2, 0, 3, 4).reshape(4 * held, width)
        scales = amax_history / format_limit
        inverse = (1.0 / scales).reshape(2, nx, 8).transpose(1, 0, 2).reshape(2 * held, 1)
        back = (scales[0] * scales[1]).reshape(nx, 8, 1, 1)
        masking = pair_mask.astype(f32).reshape(chunks, 1, lanes)
        vmem = pl.BlockSpec(memory_space=pltpu.VMEM)
        dma = pltpu.SemaphoreType.DMA
        update, amax = pl.pallas_call(
            functools.partial(kernel, (nz, nx, chunks)),
            out_shape=(
                jax.ShapeDtypeStruct((ni, nj, held), bf16),
                jax.ShapeDtypeStruct((2, held), f32),
            ),
            in_specs=[vmem] * 11,
            out_specs=(vmem, vmem),
            scratch_shapes=[
                pltpu.VMEM((ni * nj, width), bf16),
                pltpu.VMEM((ni * nj, held), f32),
                pltpu.VMEM((2 * held, 128), f32),
                pltpu.VMEM((chunks, nx, 16, lanes), bf16),
                pltpu.VMEM((chunks, nx, 16, lanes), bf16),
                pltpu.VMEM((16 * 40, 128), f32),
                pltpu.VMEM((16, chunks, 8, lanes), bf16),
                pltpu.VMEM((chunks, nz, 8, lanes), bf16),
                pltpu.VMEM((chunks * 128, lanes), bf16),
                pltpu.VMEM((chunks, 8, 8, lanes), bf16),
                pltpu.VMEM((chunks, 8, 8, lanes), bf16),
                pltpu.VMEM((chunks, 8, 8, lanes), bf16),
                pltpu.VMEM((8 * 40, 128), f32),
                pltpu.VMEM((chunks, nx, 8, lanes), bf16),
                pltpu.VMEM((chunks, 2, nx, 8, lanes), bf16),
                pltpu.VMEM((nx, 1, 128), f32),
                pltpu.VMEM((nz, 1, 128), f32),
                dma((chunks, nx)),
                dma((chunks, nx)),
                dma((chunks, nz)),
                dma((chunks, nz)),
                dma((chunks, 8)),
                dma((chunks, 8)),
                dma((chunks, 8)),
                dma((chunks, 8)),
                dma((chunks, nx)),
                dma((chunks, nx)),
                dma((chunks,)),
                dma((chunks,)),
                dma((nx,)),
                dma((nx,)),
                dma((nz,)),
                dma((nz,)),
            ],
            compiler_params=pltpu.CompilerParams(
                collective_id=0, has_side_effects=True, vmem_limit_bytes=48 * 2**20
            ),
            name="triangle",
        )(
            pair_rep[0],
            masking,
            weights,
            inverse,
            back,
            in_gain[None],
            in_bias[None],
            gate_weight,
            out_gain[:, None],
            out_bias[:, None],
            out_weight,
        )
        return update[None], amax

    placed = (
        P("ga", "gx", "gy", None),
        P("ga", "gx", "gy"),
        P(None, "col"),
        P(),
        P(),
        P(None, None, "col"),
        P(None, "col"),
        P(),
        P(),
        P(None, "col"),
    )
    return jax.shard_map(
        on_device,
        mesh=mesh,
        in_specs=placed,
        out_specs=(P("ga", "gx", "gy", "col"), P("ga", "col")),
        check_vma=False,
    )
```

time: 404 us -> 135 us (0.33)
  blocking collectives: 200 us -> 0 us
  Pallas kernels: 0 us -> 126 us
  waiting for transfers between devices: 118 us -> 0 us
  local copies, waits for them, and re-layouts: 39.4 us -> 7.91 us
  other arithmetic: 16.5 us -> 0.03 us
  between operations: 14.3 us -> 0.72 us
  matrix products: 10.7 us -> 0 us
  starting transfers between devices: 4.97 us -> 0 us
    all_gather x2 -> x0, blocking collectives: 200 us -> none  [the longest x1 185 us: total_of_pieces(): parts = lax.all_gather(array, axis)]
    pallas_call x0 -> x1, Pallas kernels: none -> 126 us  [on_device(): pl.pallas_call(functools.partial(kernel, (nz, nx, chunks)), out_shape=(ja...]
    all_gather x1 -> x0, waiting for transfers between devices: 117 us -> none  [crop_triangle(): wide_rows = lax.all_gather(right_q, 'gy', axis=2, tiled=True)]
    all_gather x1 -> x0, local copies, waits for them, and re-layouts: 14.6 us -> none  [crop_triangle(): wide_rows = lax.all_gather(right_q, 'gy', axis=2, tiled=True)]
    transpose x1, local copies, waits for them, and re-layouts: 10.9 us -> 0.01 us  [on_device(): (1.0 / scales).reshape(2, nx, 8).transpose(1, 0, 2).reshape(2 * held, 1)]
    dot_general x4 -> x0, matrix products: 10.7 us -> none  [the longest x1 5.11 us: crop_triangle(): jnp.einsum('cik,cjk->cij', gather_directly(left_q, 'gy', 2), panel, prefe...]
    reshape x1 -> x4, local copies, waits for them, and re-layouts: 7.16 us -> 0.27 us  [the longest x2 0.17 us: on_device(): (1.0 / scales).reshape(2, nx, 8).transpose(1, 0, 2).reshape(2 * held, 1)]
    unnamed x24, local copies, waits for them, and re-layouts: 2.02 us -> 7.24 us
  transfers between devices with their start and end apart: 3 -> 0, of which waited for: 1 -> 0; matrix products, arithmetic and copies ran while one was open for 7% -> 0% of each run, Pallas kernels for 0% -> 0%
where the time goes in v1:
time: 135 us
  Pallas kernels  126 us (93%)
  local copies, waits for them, and re-layouts  7.91 us (6%)
    pallas_call x1, Pallas kernels, on_device(): pl.pallas_call(functools.partial(kernel, (nz, nx, chunks)), out_shape=(ja...  126 us
    unnamed x24, local copies, waits for them, and re-layouts  7.24 us

profile of v1, /device:TPU:65, one launch (start us, length us, event | category | flops | bytes accessed | tf_op | source)
XLA Modules:
  0.0 135.0 jit_solution(6374405439863816376)
XLA Ops:
  0.6 0.0 copy-start.7
  0.6 0.0 copy-start.4
  0.6 0.7 copy-done.7
  1.3 0.1 reshape.41
  1.4 0.0 copy-done.4
  1.4 0.1 reshape.38.mask_ref
  1.5 0.0 copy-start.5
  1.6 0.2 mul.15.back_ref
  1.7 0.5 copy-done.5
  2.3 0.0 copy-start.6
  2.3 0.1 copy.16.gate_w_ref
  2.4 0.6 copy-done.6
  3.0 0.0 copy-start.3
  3.0 0.1 copy.19.out_w_ref
  3.1 0.1 reshape.43.inv_ref
  3.2 0.6 copy-done.3
  3.8 0.0 copy-start.8
  3.8 0.6 copy-done.8
  4.5 0.0 copy-start.9
  4.5 0.1 copy.17.out_gain_ref
  4.6 0.5 copy-done.9
  5.1 0.0 copy-start.1
  5.2 0.0 copy-start.2
  5.2 0.1 copy.18.out_bias_ref
  5.3 0.5 copy-done.1
  5.8 0.0 copy-done.2
  5.8 0.0 copy-start
  5.8 1.1 copy-done
  7.0 126.3 %triangle.1 = (bf16[40,80,64]{2,1,0:T(8,128)(2,1)S(1)}, f32[2,64]{1,0:T(2,128)S(1)}) custom-call(bf16[40,80,128]{2,1,0:T(8,128)(2,1)S(1)} %bitcast.13, f32[5,1,640]{2,1,0:T(1,128)S(1)} %reshape.38.mask_ref, bf16[256,128]{1,0:T(8,128)(2,1)S(1)} %bitcast.15, f32[128,1]{1,0:T(8,128)S(1)} %reshape.43.inv_ref, f32[8,8,1,1]{3,2,1,0:T(1,128)S(1)} %mul.15.back_ref, ...), custom_call_target="tpu_custom_call" | custom-call | tf_op jit(solution)/shard_map/triangle/pallas_call | solution.py:325
  133.3 1.1 copy.20
  134.4 0.6 copy.22
  (5 shorter events, 0.0 us)
Async XLA Ops:
  0.6 0.7 copy-start.7
  0.6 0.8 copy-start.4
  1.5 0.7 copy-start.5
  2.3 0.7 copy-start.6
  3.0 0.8 copy-start.3
  3.8 0.7 copy-start.8
  4.5 0.7 copy-start.9
  5.1 0.7 copy-start.1
  5.2 0.7 copy-start.2
  5.8 1.1 copy-start

commit v2 on v0

v2 whole, which is shorter than its diff:
```python
import functools

import jax
import jax.numpy as jnp
from jax import lax
from jax.experimental import pallas as pl
from jax.experimental.pallas import tpu as pltpu
from jax.sharding import PartitionSpec as P

epsilon = 1e-05
format_limit = 448.0
MESH = pl.DeviceIdType.MESH
f32, bf16 = jnp.float32, jnp.bfloat16


def block_transpose(parts):
    parts = list(parts)
    shape = parts[0].shape
    block = lax.broadcasted_iota(jnp.int32, shape, len(shape) - 1) // 16
    for bit in (4, 2, 1):
        low = (block & bit) == 0
        for a in range(8):
            if a & bit:
                continue
            x, y = parts[a], parts[a | bit]
            parts[a] = jnp.where(low, x, pltpu.roll(y, 16 * bit, 1))
            parts[a | bit] = jnp.where(low, pltpu.roll(x, 128 - 16 * bit, 1), y)
    return parts


def kernel(sizes, *refs):
    nz, nx, chunks, names = sizes
    ref = dict(zip(names, refs))
    z, x, core = lax.axis_index("gx"), lax.axis_index("gy"), lax.axis_index("col")
    other = 1 - core
    half = nz // 2
    slot = lax.rem(z, half)
    lanes = 640

    def column(row, width):
        return jnp.broadcast_to(row, (width, row.shape[1])).T

    def load(name):
        return pltpu.make_async_copy(ref[name + "_h"], ref[name], ref["in_sem"].at[inputs.index(name)])

    inputs = [n[:-2] for n in names if n.endswith("_h") and n != "pair_h"]

    def pair_load(c):
        return pltpu.make_async_copy(
            ref["pair_h"].at[0, pl.ds(8 * c, 8)], ref["pair"].at[pl.ds(8 * c, 8)], ref["pair_sem"].at[c]
        )

    def send(src, dst, ss, rs, target):
        pltpu.make_async_remote_copy(
            src_ref=src, dst_ref=dst, send_sem=ss, recv_sem=rs, device_id=target, device_id_type=MESH
        ).start()

    def await_bytes(like, sem):
        pltpu.make_async_copy(like, like, sem).wait()

    def zp(d):
        return lax.rem(z + d, nz)

    def xp(d):
        return lax.rem(x + d, nx)

    rank = lax.rem(z + nz - 1, nz)

    def ranked(r):
        return lax.rem(r + 1, nz)

    def each(low, high, body):
        def step(i, carry):
            body(i)
            return carry

        lax.fori_loop(low, high, step, 0)

    barrier = pltpu.get_barrier_semaphore()
    for d in range(1, nx):
        pl.semaphore_signal(barrier, inc=1, device_id={"gy": xp(d)}, device_id_type=MESH)
    pl.semaphore_signal(barrier, inc=1, device_id={"col": other}, device_id_type=MESH)
    each(
        rank + 1,
        nz,
        lambda r: pl.semaphore_signal(
            barrier, inc=1, device_id={"gx": ranked(r)}, device_id_type=MESH
        ),
    )
    for name in inputs[:6]:
        load(name).start()
    for c in range(chunks):
        pair_load(c).start()
    for name in inputs[6:]:
        load(name).start()
    with jax.named_scope("input"):
        for name in inputs:
            load(name).wait()

    x_order = []
    for d in range(nx // 2, 0, -1):
        x_order.append(d)
        if nx - d != d:
            x_order.append(nx - d)

    def x_send(kind, c):
        for d in x_order:
            t = xp(d)
            send(
                ref["xs" + kind].at[c, t],
                ref["xr" + kind].at[c, x],
                ref[f"xs{kind}_ss"].at[0],
                ref[f"xs{kind}_rs"].at[c],
                {"gy": t},
            )

    history = ref["history"][...]
    inverse = format_limit / history
    inverse_left = column(inverse[0:1, :], 128)
    inverse_right = column(inverse[1:2, :], 128)
    weights = ref["w"][...].reshape(256, 128)
    for c in range(chunks):
        with jax.named_scope("pair"):
            pair_load(c).wait()
        with jax.named_scope("norm"):
            rows = ref["pair"][8 * c : 8 * c + 8].reshape(lanes, 128).astype(f32)
            average = jnp.mean(rows, axis=-1, keepdims=True)
            centred = rows - average
            spread = jnp.mean(centred * centred, axis=-1, keepdims=True)
            flat = (
                centred * lax.rsqrt(spread + epsilon) * ref["gain"][...] + ref["bias"][...]
            ).astype(bf16)
            ref["normed"][lanes * c : lanes * c + lanes, :] = flat
            kept = ref["mask"][0, 8 * c : 8 * c + 8, :].astype(f32).T
            masked = jnp.concatenate(
                [flat[80 * i : 80 * i + 80] * kept[:, i : i + 1].astype(bf16) for i in range(8)], axis=0
            )
            proj = lax.dot_general(
                weights, masked, (((1,), (1,)), ((), ())), preferred_element_type=f32
            )
        with jax.named_scope("quant"):
            for kind, base, inv in (("r", 128, inverse_right), ("l", 0, inverse_left)):
                both = jax.nn.sigmoid(proj[base + 64 : base + 128]) * proj[base : base + 64]
                tiles = [both[:, 128 * k : 128 * k + 128] for k in range(5)]
                top = functools.reduce(jnp.maximum, [jnp.abs(tile) for tile in tiles])
                peak = ref["peak" + kind]
                peak[...] = top if c == 0 else jnp.maximum(peak[...], top)
                quant = jnp.concatenate(
                    [jnp.clip(tile * inv, -format_limit, format_limit) for tile in tiles], axis=1
                )
                ref["xs" + kind][c] = quant.astype(bf16).reshape(8, 8, lanes)
                ref["xr" + kind][c, x] = ref["xs" + kind][c, x]
                if kind == "r":
                    if c == 0:
                        with jax.named_scope("entry"):
                            pl.semaphore_wait(barrier, nx + rank)
                        each(
                            0,
                            rank,
                            lambda r: pl.semaphore_signal(
                                ref["known"].at[z], inc=1, device_id={"gx": ranked(r)}, device_id_type=MESH
                            ),
                        )
                    x_send("r", c)
    for c in range(chunks):
        x_send("l", c)
    with jax.named_scope("peak"):
        tops = jnp.concatenate([ref["peakl"][...], ref["peakr"][...]], axis=0)
        ref["peak_x"][x] = jnp.max(tops.T, axis=0, keepdims=True)
        for d in x_order:
            send(
                ref["peak_x"].at[x],
                ref["peak_x"].at[x],
                ref["px_ss"].at[0],
                ref["px_rs"].at[0],
                {"gy": xp(d)},
            )
    with jax.named_scope("gate"):
        for c in range(chunks):
            ref["gates"][c] = jax.nn.sigmoid(
                lax.dot_general(
                    ref["gate_w"][...],
                    ref["normed"][lanes * c : lanes * c + lanes, :],
                    (((1,), (1,)), ((), ())),
                    preferred_element_type=f32,
                )
            )

    def gather_rows(kind, c):
        with jax.named_scope("xwait" + kind):
            await_bytes(ref["xr" + kind].at[c, pl.ds(0, nx - 1)], ref[f"xs{kind}_rs"].at[c])
        staged = ref["staged"]
        with jax.named_scope("relay" + kind):
            for g in range(5):
                parts = [
                    ref["xr" + kind][c, a, :, 128 * g : 128 * g + 128].astype(f32) for a in range(8)
                ]
                for p, part in enumerate(block_transpose(parts)):
                    staged[8 * (8 * g + p) : 8 * (8 * g + p) + 8, :] = part
            for s in range(8):
                tiles = [staged[pl.ds(8 * k + s, 8, stride=40), :] for k in range(5)]
                ref["ready" + kind][s, c] = jnp.concatenate(tiles, axis=1).astype(bf16)

    def send_right(c, t):
        send(
            ref["readyr"].at[lax.rem(t, half), c],
            ref["rhome"].at[z, c],
            ref["r_ss"].at[0],
            ref["r_rs"].at[z],
            {"gx": t},
        )

    def send_left(c, t):
        send(
            ref["readyl"].at[lax.rem(t, half), c],
            ref["lhome"].at[slot, c],
            ref["l_ss"].at[0],
            ref["l_rs"].at[slot],
            {"gx": t},
        )

    def in_arc(t):
        e = lax.rem(t - z + nz, nz)
        return (e < half // 2) | (e > nz - half // 2) | (e == half // 2 + half * core)

    def send_peak(t):
        send(
            ref["peak_z"].at[z], ref["peak_z"].at[z], ref["pz_ss"].at[0], ref["pz_rs"].at[0], {"gx": t}
        )

    ahead = half // 2
    near = lax.min(rank + 1 + ahead, nz)

    def left_to(r):
        t = ranked(r)

        @pl.when(in_arc(t))
        def _():
            for c in range(chunks):
                send_left(c, t)

    def right_to(r):
        t = ranked(r)
        pl.semaphore_wait(ref["known"].at[t], 1)
        for c in range(chunks):
            send_right(c, t)

    def rest_to(r):
        right_to(r)
        left_to(r)
        send_peak(ranked(r))

    for c in range(chunks):
        gather_rows("r", c)
        ref["rhome"][z, c] = ref["readyr"][slot, c]
        each(0, rank, lambda r: send_right(c, ranked(r)))
    with jax.named_scope("near"):
        each(rank + 1, near, right_to)
    for c in range(chunks):
        gather_rows("l", c)
        ref["lhome"][slot, c] = ref["readyl"][slot, c]

        def left_below(r):
            t = ranked(r)

            @pl.when(in_arc(t))
            def _():
                send_left(c, t)

        each(0, rank, left_below)
    each(rank + 1, near, left_to)
    with jax.named_scope("peakwait"):
        await_bytes(ref["peak_x"].at[pl.ds(0, nx - 1)], ref["px_rs"].at[0])
    ref["peak_z"][z] = jnp.max(ref["peak_x"][...], axis=0)
    each(0, rank, lambda r: send_peak(ranked(r)))
    each(rank + 1, near, lambda r: send_peak(ranked(r)))
    with jax.named_scope("higher"):
        each(near, nz, rest_to)
    with jax.named_scope("sentx"):
        await_bytes(ref["peak_x"].at[pl.ds(0, nx - 1)], ref["px_ss"].at[0])
        await_bytes(ref["lhome"].at[pl.ds(0, nx - 1)], ref["xsr_ss"].at[0])
        await_bytes(ref["lhome"].at[pl.ds(0, nx - 1)], ref["xsl_ss"].at[0])

    def right_arrived(n):
        source = zp(n)
        await_bytes(ref["rhome"].at[source], ref["r_rs"].at[source])

    with jax.named_scope("rightwait"):
        each(1, nz, right_arrived)
    with jax.named_scope("rmat"):
        for t in range(5):
            granules = []
            for b in range(8):
                for g in (2 * t, 2 * t + 1):
                    granules.append(ref["rhome"][2 * b + g // 5, g % 5].astype(f32))
            ref["rmat"][128 * t : 128 * t + 128, :] = jnp.concatenate(granules, axis=0).astype(bf16)

    product_scale = history[0:1, :] * history[1:2, :] * (1.0 / format_limit / format_limit)
    channel = 8 * x + slot
    here = lax.broadcasted_iota(jnp.int32, product_scale.shape, 1) == channel
    back = jnp.sum(jnp.where(here, product_scale, 0.0), axis=1, keepdims=True)
    first = lax.rem(rank - half // 2 + core + nz, nz)
    turn = jnp.where(first > half, nz - first, 0)

    def triangle(n):
        row = ranked(lax.rem(first + lax.rem(turn + n, half), nz))
        place = lax.rem(row, half)

        with jax.named_scope("leftwait"):
            @pl.when(row != z)
            def _():
                await_bytes(ref["lhome"].at[place], ref["l_rs"].at[place])

        with jax.named_scope("dot"):
            left = ref["lhome"][place].astype(f32).reshape(40, lanes).astype(bf16)
            product = lax.dot_general(
                left, ref["rmat"][...], (((1,), (1,)), ((), ())), preferred_element_type=f32
            )
            ref["tsend"][place] = (product * back).reshape(chunks, 8, lanes).astype(bf16)

        @pl.when(row == z)
        def _():
            for c in range(chunks):
                ref["trecv"][c, slot] = ref["tsend"][place, c]

        @pl.when(row != z)
        def _():
            for c in range(chunks):
                send(
                    ref["tsend"].at[place, c],
                    ref["trecv"].at[c, slot],
                    ref["t_ss"].at[0],
                    ref["t_rs"].at[c],
                    {"gx": row},
                )

    each(0, half, triangle)

    with jax.named_scope("sent"):
        await_bytes(ref["rhome"].at[pl.ds(0, nz - 1)], ref["r_ss"].at[0])
        await_bytes(ref["lhome"].at[pl.ds(0, half - 1)], ref["l_ss"].at[0])
        await_bytes(ref["peak_z"].at[pl.ds(0, nz - 1)], ref["pz_ss"].at[0])
        await_bytes(ref["peak_z"].at[pl.ds(0, nz - 1)], ref["pz_rs"].at[0])
    tops = jnp.max(ref["peak_z"][...], axis=0)
    ref["amax"][0:1, :] = tops[:, :64]
    ref["amax"][1:2, :] = tops[:, 64:]

    def over_x(c):
        with jax.named_scope("triwait"):
            await_bytes(ref["trecv"].at[c, pl.ds(0, half - 1)], ref["t_rs"].at[c])
        staged = ref["staged"]
        with jax.named_scope("relayt"):
            for s in range(8):
                for j in range(5):
                    staged[pl.ds(8 * j + s, 8, stride=40), :] = ref["trecv"][
                        c, s, :, 128 * j : 128 * j + 128
                    ].astype(f32)
            for g in range(5):
                parts = [staged[8 * (8 * g + p) : 8 * (8 * g + p) + 8, :] for p in range(8)]
                for b, part in enumerate(block_transpose(parts)):
                    ref["txsend"][c, b, :, 128 * g : 128 * g + 128] = part.astype(bf16)
            ref["tfull"][c, core, x] = ref["txsend"][c, x]
            for d in x_order:
                t = xp(d)
                send(
                    ref["txsend"].at[c, t],
                    ref["tfull"].at[c, core, x],
                    ref["tx_ss"].at[0],
                    ref["tx_rs"].at[c],
                    {"gy": t},
                )

    def over_core(c):
        with jax.named_scope("colwait"):
            await_bytes(ref["tfull"].at[c, core, pl.ds(0, nx - 1)], ref["tx_rs"].at[c])
        send(
            ref["tfull"].at[c, core],
            ref["tfull"].at[c, core],
            ref["d_ss"].at[0],
            ref["d_rs"].at[c],
            {"col": other},
        )

    out_gain = column(ref["out_gain"][...], 128)
    out_bias = column(ref["out_bias"][...], 128)

    def finish(c):
        with jax.named_scope("corewait"):
            await_bytes(ref["tfull"].at[c, other], ref["d_rs"].at[c])
        with jax.named_scope("finish"):
            values = ref["tfull"][c].astype(f32).reshape(128, lanes)
            average = jnp.mean(values, axis=0, keepdims=True)
            centred = values - average
            spread = jnp.mean(centred * centred, axis=0, keepdims=True)
            scaled = centred * lax.rsqrt(spread + epsilon)
            tnorm = jnp.concatenate(
                [scaled[:, 128 * k : 128 * k + 128] * out_gain + out_bias for k in range(5)], axis=1
            ).astype(bf16)
            mixing = jnp.dot(ref["out_w"][...], tnorm, preferred_element_type=f32)
            update = ref["gates"][c] * mixing
            for i in range(8):
                ref["held"][8 * c + i] = update[:, 80 * i : 80 * i + 80].astype(bf16)

    def store(c):
        block = pl.ds(8 * c, 8)
        return pltpu.make_async_copy(ref["held"].at[block], ref["out"].at[block], ref["out_sem"].at[c])

    for c in range(chunks):
        over_x(c)
    with jax.named_scope("sent2"):
        await_bytes(ref["tsend"].at[pl.ds(0, half - 1)], ref["t_ss"].at[0])
    for c in range(chunks + 1):
        if c < chunks:
            over_core(c)
        if c > 0:
            finish(c - 1)
            store(c - 1).start()
    await_bytes(ref["lhome"].at[pl.ds(0, nx - 1)], ref["tx_ss"].at[0])
    await_bytes(ref["lhome"], ref["d_ss"].at[0])
    for c in range(chunks):
        store(c).wait()


def solution(mesh):
    nz, nx = mesh.shape["gx"], mesh.shape["gy"]

    def on_device(
        pair_rep,
        pair_mask,
        amax_history,
        in_gain,
        in_bias,
        proj_weight,
        gate_weight,
        out_gain,
        out_bias,
        out_weight,
    ):
        _, ni, nj, width = pair_rep.shape
        held = proj_weight.shape[2]
        chunks = ni // 8
        lanes = 8 * nj
        half = nz // 2
        assert nx == 8 and nz == 16 and lanes == 640 and width == 128 and held == 64
        dma = pltpu.SemaphoreType.DMA
        operands = {
            "mask_h": pair_mask,
            "history_h": amax_history,
            "w_h": proj_weight.transpose(1, 2, 0),
            "gain_h": in_gain[None],
            "bias_h": in_bias[None],
            "gate_w_h": gate_weight.T,
            "out_gain_h": out_gain[None],
            "out_bias_h": out_bias[None],
            "out_w_h": out_weight.T,
            "pair_h": pair_rep,
        }
        scratch = {
            name[:-2]: pltpu.VMEM(value.shape, value.dtype)
            for name, value in operands.items()
            if name != "pair_h"
        }
        scratch.update(
            pair=pltpu.VMEM((ni, nj, width), bf16),
            held=pltpu.VMEM((ni, held, nj), bf16),
            out_sem=dma((chunks,)),
            in_sem=dma((len(operands) - 1,)),
            pair_sem=dma((chunks,)),
            normed=pltpu.VMEM((ni * nj, width), bf16),
            gates=pltpu.VMEM((chunks, held, lanes), f32),
            peakl=pltpu.VMEM((held, 128), f32),
            peakr=pltpu.VMEM((held, 128), f32),
            xsr=pltpu.VMEM((chunks, nx, 8, lanes), bf16),
            xsl=pltpu.VMEM((chunks, nx, 8, lanes), bf16),
            xrr=pltpu.VMEM((chunks, nx, 8, lanes), bf16),
            xrl=pltpu.VMEM((chunks, nx, 8, lanes), bf16),
            staged=pltpu.VMEM((8 * 40, 128), f32),
            readyr=pltpu.VMEM((8, chunks, 8, lanes), bf16),
            readyl=pltpu.VMEM((8, chunks, 8, lanes), bf16),
            rhome=pltpu.VMEM((nz, chunks, 8, lanes), bf16),
            rmat=pltpu.VMEM((lanes, lanes), bf16),
            lhome=pltpu.VMEM((half, chunks, 8, lanes), bf16),
            tsend=pltpu.VMEM((half, chunks, 8, lanes), bf16),
            trecv=pltpu.VMEM((chunks, half, 8, lanes), bf16),
            txsend=pltpu.VMEM((chunks, nx, 8, lanes), bf16),
            tfull=pltpu.VMEM((chunks, 2, nx, 8, lanes), bf16),
            peak_x=pltpu.VMEM((nx, 1, 128), f32),
            peak_z=pltpu.VMEM((nz, 1, 128), f32),
            known=pltpu.SemaphoreType.REGULAR((nz,)),
            px_ss=dma((1,)),
            px_rs=dma((1,)),
            pz_ss=dma((1,)),
            pz_rs=dma((1,)),
            xsr_ss=dma((1,)),
            xsr_rs=dma((chunks,)),
            xsl_ss=dma((1,)),
            xsl_rs=dma((chunks,)),
            r_ss=dma((1,)),
            r_rs=dma((nz,)),
            l_ss=dma((1,)),
            l_rs=dma((half,)),
            t_ss=dma((1,)),
            t_rs=dma((chunks,)),
            tx_ss=dma((1,)),
            tx_rs=dma((chunks,)),
            d_ss=dma((1,)),
            d_rs=dma((chunks,)),
        )
        names = (*operands, "out", "amax", *scratch)
        vmem = pl.BlockSpec(memory_space=pltpu.VMEM)
        update, amax = pl.pallas_call(
            functools.partial(kernel, (nz, nx, chunks, names)),
            out_shape=(
                jax.ShapeDtypeStruct((ni, held, nj), bf16),
                jax.ShapeDtypeStruct((2, held), f32),
            ),
            in_specs=[pl.BlockSpec(memory_space=pltpu.HBM)] * len(operands),
            out_specs=(pl.BlockSpec(memory_space=pltpu.HBM), vmem),
            scratch_shapes=list(scratch.values()),
            compiler_params=pltpu.CompilerParams(
                collective_id=0, has_side_effects=True, vmem_limit_bytes=67_043_328
            ),
            name="triangle",
        )(*operands.values())
        return update.transpose(0, 2, 1)[None], amax

    placed = (
        P("ga", "gx", "gy", None),
        P("ga", "gx", "gy"),
        P(None, "col"),
        P(),
        P(),
        P(None, None, "col"),
        P(None, "col"),
        P(),
        P(),
        P(None, "col"),
    )
    return jax.shard_map(
        on_device,
        mesh=mesh,
        in_specs=placed,
        out_specs=(P("ga", "gx", "gy", "col"), P("ga", "col")),
        check_vma=False,
    )
```

time: 404 us -> 121 us (0.30)
  blocking collectives: 200 us -> 0 us
  Pallas kernels: 0 us -> 118 us
  waiting for transfers between devices: 118 us -> 0 us
  local copies, waits for them, and re-layouts: 39.4 us -> 2.53 us
  other arithmetic: 16.5 us -> 0 us
  between operations: 14.3 us -> 0.65 us
  matrix products: 10.7 us -> 0 us
  starting transfers between devices: 4.97 us -> 0 us
    all_gather x2 -> x0, blocking collectives: 200 us -> none  [the longest x1 185 us: total_of_pieces(): parts = lax.all_gather(array, axis)]
    pallas_call x0 -> x1, Pallas kernels: none -> 118 us  [on_device(): pl.pallas_call(functools.partial(kernel, (nz, nx, chunks, names)), out_sh...]
    all_gather x1 -> x0, waiting for transfers between devices: 117 us -> none  [crop_triangle(): wide_rows = lax.all_gather(right_q, 'gy', axis=2, tiled=True)]
    all_gather x1 -> x0, local copies, waits for them, and re-layouts: 14.6 us -> none  [crop_triangle(): wide_rows = lax.all_gather(right_q, 'gy', axis=2, tiled=True)]
    transpose x1 -> x0, local copies, waits for them, and re-layouts: 10.9 us -> none  [joined_along(): return jnp.moveaxis(parts, 0, dim).reshape(dims)]
    dot_general x4 -> x0, matrix products: 10.7 us -> none  [the longest x1 5.11 us: crop_triangle(): jnp.einsum('cik,cjk->cij', gather_directly(left_q, 'gy', 2), panel, prefe...]
    reshape x1 -> x0, local copies, waits for them, and re-layouts: 7.16 us -> none  [joined_along(): return jnp.moveaxis(parts, 0, dim).reshape(dims)]
    all_to_all x1 -> x0, starting transfers between devices: 4.84 us -> none  [copy_for_each(): return lax.all_to_all(copies, axis, split_axis=0, concat_axis=0, tiled=True)]
  transfers between devices with their start and end apart: 3 -> 0, of which waited for: 1 -> 0; matrix products, arithmetic and copies ran while one was open for 7% -> 0% of each run, Pallas kernels for 0% -> 0%
where the time goes in v2:
time: 121 us
  Pallas kernels  118 us (98%)
  local copies, waits for them, and re-layouts  2.53 us (2%)
    pallas_call x1, Pallas kernels, on_device(): pl.pallas_call(functools.partial(kernel, (nz, nx, chunks, names)), out_sh...  118 us
    unnamed x4, local copies, waits for them, and re-layouts  2.53 us

profile of v2, /device:TPU:65, one launch (start us, length us, event | category | flops | bytes accessed | tf_op | source)
XLA Modules:
  0.0 120.8 jit_solution(991629086308338731)
XLA Ops:
  0.6 117.6 %triangle.1 = (bf16[40,64,80]{2,1,0:T(8,128)(2,1)}, f32[2,64]{1,0:T(2,128)}) custom-call(s32[1,40,80]{2,1,0:T(8,128)} %refs_0_.1, f32[2,64]{1,0:T(2,128)} %refs_1_.1, bf16[4,64,128]{2,1,0:T(8,128)(2,1)} %bitcast.11, f32[1,128]{1,0:T(1,128)} %bitcast.14, f32[1,128]{1,0:T(1,128)} %bitcast.15, bf16[64,128]{1,0:T(8,128)(2,1)} %bitcast.12, f32[1,128]{1,0:T(1,128)} %bitcast.16, ...), custom_call_target="tpu_custom_call" | custom-call | tf_op jit(solution)/shard_map/triangle/pallas_call | solution.py:511
  118.3 0.0 copy-start
  118.3 2.0 %copy.14 = bf16[1,40,80,64]{2,3,1,0:T(8,128)(2,1)} copy(bf16[1,40,80,64]{2,3,1,0:T(8,128)(2,1)} %bitcast.10) | data formatting | bytes 819200
  120.3 0.0 copy-done
  120.3 0.6 copy.15
Async XLA Ops:
  118.3 2.0 %copy-start = (f32[2,64]{1,0:T(2,128)S(1)}, f32[2,64]{1,0:T(2,128)}, u32[]{:S(2)}) copy-start(f32[2,64]{1,0:T(2,128)} %get-tuple-element.9) | copy-start | bytes 1540

commit v3 on v2

--- a/solution.py
+++ b/solution.py
@@ -93,6 +93,22 @@
         pair_load(c).start()
     for name in inputs[6:]:
         load(name).start()
+
+    def enter():
+        with jax.named_scope("entry"):
+            pl.semaphore_wait(barrier, nx + rank)
+        each(
+            0,
+            rank,
+            lambda r: pl.semaphore_signal(
+                ref["known"].at[z], inc=1, device_id={"gx": ranked(r)}, device_id_type=MESH
+            ),
+        )
+
+    @pl.when(rank < nz - 1)
+    def _():
+        enter()
+
     with jax.named_scope("input"):
         for name in inputs:
             load(name).wait()
@@ -152,15 +168,11 @@
                 ref["xr" + kind][c, x] = ref["xs" + kind][c, x]
                 if kind == "r":
                     if c == 0:
-                        with jax.named_scope("entry"):
-                            pl.semaphore_wait(barrier, nx + rank)
-                        each(
-                            0,
-                            rank,
-                            lambda r: pl.semaphore_signal(
-                                ref["known"].at[z], inc=1, device_id={"gx": ranked(r)}, device_id_type=MESH
-                            ),
-                        )
+
+                        @pl.when(rank == nz - 1)
+                        def _():
+                            enter()
+
                     x_send("r", c)
     for c in range(chunks):
         x_send("l", c)
@@ -215,7 +227,7 @@
             ref["readyl"].at[lax.rem(t, half), c],
             ref["lhome"].at[slot, c],
             ref["l_ss"].at[0],
-            ref["l_rs"].at[slot],
+            ref["l_rs"].at[0],
             {"gx": t},
         )
 
@@ -228,7 +240,7 @@
             ref["peak_z"].at[z], ref["peak_z"].at[z], ref["pz_ss"].at[0], ref["pz_rs"].at[0], {"gx": t}
         )
 
-    ahead = half // 2
+    ahead = half - 2
     near = lax.min(rank + 1 + ahead, nz)
 
     def left_to(r):
@@ -299,42 +311,33 @@
     channel = 8 * x + slot
     here = lax.broadcasted_iota(jnp.int32, product_scale.shape, 1) == channel
     back = jnp.sum(jnp.where(here, product_scale, 0.0), axis=1, keepdims=True)
-    first = lax.rem(rank - half // 2 + core + nz, nz)
-    turn = jnp.where(first > half, nz - first, 0)
-
-    def triangle(n):
-        row = ranked(lax.rem(first + lax.rem(turn + n, half), nz))
-        place = lax.rem(row, half)
-
-        with jax.named_scope("leftwait"):
-            @pl.when(row != z)
-            def _():
-                await_bytes(ref["lhome"].at[place], ref["l_rs"].at[place])
-
+    first = z - half // 2 + core + nz
+    with jax.named_scope("leftwait"):
+        await_bytes(ref["lhome"].at[pl.ds(0, half - 1)], ref["l_rs"].at[0])
+
+    for c in range(chunks):
         with jax.named_scope("dot"):
-            left = ref["lhome"][place].astype(f32).reshape(40, lanes).astype(bf16)
+            left = jnp.concatenate(
+                [ref["lhome"][place, c].astype(f32) for place in range(half)], axis=0
+            ).astype(bf16)
             product = lax.dot_general(
                 left, ref["rmat"][...], (((1,), (1,)), ((), ())), preferred_element_type=f32
             )
-            ref["tsend"][place] = (product * back).reshape(chunks, 8, lanes).astype(bf16)
-
-        @pl.when(row == z)
-        def _():
-            for c in range(chunks):
-                ref["trecv"][c, slot] = ref["tsend"][place, c]
-
-        @pl.when(row != z)
-        def _():
-            for c in range(chunks):
-                send(
-                    ref["tsend"].at[place, c],
-                    ref["trecv"].at[c, slot],
-                    ref["t_ss"].at[0],
-                    ref["t_rs"].at[c],
-                    {"gx": row},
-                )
-
-    each(0, half, triangle)
+            ref["tsend"][c] = (product * back).reshape(half, 8, lanes).astype(bf16)
+        ref["trecv"][c, slot] = ref["tsend"][c, slot]
+
+        def triangle(n):
+            place = lax.rem(slot + n, half)
+            row = lax.rem(first + lax.rem(place - lax.rem(first, half) + half, half), nz)
+            send(
+                ref["tsend"].at[c, place],
+                ref["trecv"].at[c, slot],
+                ref["t_ss"].at[0],
+                ref["t_rs"].at[c],
+                {"gx": row},
+            )
+
+        each(1, half, triangle)
 
     with jax.named_scope("sent"):
         await_bytes(ref["rhome"].at[pl.ds(0, nz - 1)], ref["r_ss"].at[0])
@@ -408,7 +411,7 @@
     for c in range(chunks):
         over_x(c)
     with jax.named_scope("sent2"):
-        await_bytes(ref["tsend"].at[pl.ds(0, half - 1)], ref["t_ss"].at[0])
+        await_bytes(ref["lhome"].at[pl.ds(0, half - 1)], ref["t_ss"].at[0])
     for c in range(chunks + 1):
         if c < chunks:
             over_core(c)
@@ -480,7 +483,7 @@
             rhome=pltpu.VMEM((nz, chunks, 8, lanes), bf16),
             rmat=pltpu.VMEM((lanes, lanes), bf16),
             lhome=pltpu.VMEM((half, chunks, 8, lanes), bf16),
-            tsend=pltpu.VMEM((half, chunks, 8, lanes), bf16),
+            tsend=pltpu.VMEM((chunks, half, 8, lanes), bf16),
             trecv=pltpu.VMEM((chunks, half, 8, lanes), bf16),
             txsend=pltpu.VMEM((chunks, nx, 8, lanes), bf16),
             tfull=pltpu.VMEM((chunks, 2, nx, 8, lanes), bf16),
@@ -498,7 +501,7 @@
             r_ss=dma((1,)),
             r_rs=dma((nz,)),
             l_ss=dma((1,)),
-            l_rs=dma((half,)),
+            l_rs=dma((1,)),
             t_ss=dma((1,)),
             t_rs=dma((chunks,)),
             tx_ss=dma((1,)),

time: 121 us -> 118 us (0.975)
  Pallas kernels: 118 us -> 115 us
    pallas_call x1, Pallas kernels: 118 us -> 115 us  [on_device(): pl.pallas_call(functools.partial(kernel, (nz, nx, chunks, names)), out_sh...]
where the time goes in v3:
time: 118 us
  Pallas kernels  115 us (97%)
  local copies, waits for them, and re-layouts  2.53 us (2%)
    pallas_call x1, Pallas kernels, on_device(): pl.pallas_call(functools.partial(kernel, (nz, nx, chunks, names)), out_sh...  115 us
    unnamed x4, local copies, waits for them, and re-layouts  2.53 us

profile of v3, /device:TPU:65, one launch (start us, length us, event | category | flops | bytes accessed | tf_op | source)
XLA Modules:
  0.0 118.1 jit_solution(6346274619775276453)
XLA Ops:
  0.6 114.9 %triangle.1 = (bf16[40,64,80]{2,1,0:T(8,128)(2,1)}, f32[2,64]{1,0:T(2,128)}) custom-call(s32[1,40,80]{2,1,0:T(8,128)} %refs_0_.1, f32[2,64]{1,0:T(2,128)} %refs_1_.1, bf16[4,64,128]{2,1,0:T(8,128)(2,1)} %bitcast.11, f32[1,128]{1,0:T(1,128)} %bitcast.14, f32[1,128]{1,0:T(1,128)} %bitcast.15, bf16[64,128]{1,0:T(8,128)(2,1)} %bitcast.12, f32[1,128]{1,0:T(1,128)} %bitcast.16, ...), custom_call_target="tpu_custom_call" | custom-call | tf_op jit(solution)/shard_map/triangle/pallas_call | solution.py:514
  115.6 0.0 copy-start
  115.6 2.0 %copy.14 = bf16[1,40,80,64]{2,3,1,0:T(8,128)(2,1)} copy(bf16[1,40,80,64]{2,3,1,0:T(8,128)(2,1)} %bitcast.10) | data formatting | bytes 819200
  117.5 0.0 copy-done
  117.5 0.6 copy.15
Async XLA Ops:
  115.6 2.0 %copy-start = (f32[2,64]{1,0:T(2,128)S(1)}, f32[2,64]{1,0:T(2,128)}, u32[]{:S(2)}) copy-start(f32[2,64]{1,0:T(2,128)} %get-tuple-element.9) | copy-start | bytes 1540

commit v4 on v3

--- a/solution.py
+++ b/solution.py
@@ -242,6 +242,11 @@
 
     ahead = half - 2
     near = lax.min(rank + 1 + ahead, nz)
+    soon = lax.min(rank + 3, nz)
+
+    def known_to(r):
+        pl.semaphore_wait(ref["known"].at[ranked(r)], 1)
+
 
     def left_to(r):
         t = ranked(r)
@@ -265,9 +270,14 @@
     for c in range(chunks):
         gather_rows("r", c)
         ref["rhome"][z, c] = ref["readyr"][slot, c]
+        if c == 1:
+            each(rank + 1, soon, known_to)
+        if c >= 1:
+            for b in (0, 1) if c == 1 else (c,):
+                each(rank + 1, soon, lambda r: send_right(b, ranked(r)))
         each(0, rank, lambda r: send_right(c, ranked(r)))
     with jax.named_scope("near"):
-        each(rank + 1, near, right_to)
+        each(soon, near, right_to)
     for c in range(chunks):
         gather_rows("l", c)
         ref["lhome"][slot, c] = ref["readyl"][slot, c]

time: 118 us -> 119 us (level)
  no operation moved by 1% of the time
where the time goes in v4:
time: 119 us
  Pallas kernels  116 us (97%)
  local copies, waits for them, and re-layouts  2.53 us (2%)
    pallas_call x1, Pallas kernels, on_device(): pl.pallas_call(functools.partial(kernel, (nz, nx, chunks, names)), out_sh...  116 us
    unnamed x4, local copies, waits for them, and re-layouts  2.53 us

profile of v4, /device:TPU:65, one launch (start us, length us, event | category | flops | bytes accessed | tf_op | source)
XLA Modules:
  0.0 119.2 jit_solution(10617522719566937921)
XLA Ops:
  0.6 116.0 %triangle.1 = (bf16[40,64,80]{2,1,0:T(8,128)(2,1)}, f32[2,64]{1,0:T(2,128)}) custom-call(s32[1,40,80]{2,1,0:T(8,128)} %refs_0_.1, f32[2,64]{1,0:T(2,128)} %refs_1_.1, bf16[4,64,128]{2,1,0:T(8,128)(2,1)} %bitcast.11, f32[1,128]{1,0:T(1,128)} %bitcast.14, f32[1,128]{1,0:T(1,128)} %bitcast.15, bf16[64,128]{1,0:T(8,128)(2,1)} %bitcast.12, f32[1,128]{1,0:T(1,128)} %bitcast.16, ...), custom_call_target="tpu_custom_call" | custom-call | tf_op jit(solution)/shard_map/triangle/pallas_call | solution.py:524
  116.7 0.0 copy-start
  116.7 2.0 %copy.14 = bf16[1,40,80,64]{2,3,1,0:T(8,128)(2,1)} copy(bf16[1,40,80,64]{2,3,1,0:T(8,128)(2,1)} %bitcast.10) | data formatting | bytes 819200
  118.6 0.0 copy-done
  118.6 0.6 copy.15
Async XLA Ops:
  116.7 2.0 %copy-start = (f32[2,64]{1,0:T(2,128)S(1)}, f32[2,64]{1,0:T(2,128)}, u32[]{:S(2)}) copy-start(f32[2,64]{1,0:T(2,128)} %get-tuple-element.9) | copy-start | bytes 1540
